TPU v7x, 256 devices: a 4x2x16 block of a 4x16x16 slice. The times are simulated.
256 devices in a mesh: frag: 2 (over y), orb: 128 (over z, x, core).
Axes of the slice: x: 4, y: 2, z: 16, core: 2. Of those that a mesh axis runs over, the one named last changes fastest.
The devices are a block of a 4x16x16 slice.
Arguments:
- slices: float32 [256, 640, 1024], P(('frag', 'orb')), parts along dimension 0, may hold values from -0.5 to 0.5
- occ_energy: float32 [256], P('frag'), parts along dimension 0, may hold values from -2 to -0.5
- virt_energy: float32 [1280], P('frag'), parts along dimension 0, may hold values from 0.3 to 3
- order: int32 [256], P('frag'), parts along dimension 0, may hold values from 0 to 127, each once
- near_keep: int32 [256], P(('frag', 'orb')), parts along dimension 0, may hold values 0 or 1
- far_keep: int32 [128], P('frag'), parts along dimension 0, may hold values 0 or 1
Outputs:
- density: float32 [256, 640, 1024], P(('frag', 'orb')), parts along dimension 0
There are 2 independent parts, one for each index of `frag`. A program takes and returns all parts, laid end to end along the dimension named above; each array names one. Nothing has to cross between parts.
Inputs may be any that keep to these rules, and one draw needn't show every extreme that they name: `order`: each position gets a different energy index.
All inputs are finite; a program needn't handle non-finite values. No bound on the sum of `near_keep` on one device may be relied on, other than what follows from the above.
Results may differ from a plain program's by a relative error of at most 0.0003.
Values sent between devices are 32-bit elements; how exact they have to be, the bound alone decides.
A program may use at most 128 MiB of HBM per device.

v0:
```python
import jax
import jax.numpy as jnp
from jax import lax
from jax.sharding import PartitionSpec as P


def passed_along(block, axis, distance):
    devices = range(lax.axis_size(axis))
    route = [((i - distance) % len(devices), i) for i in devices]
    return lax.ppermute(block, axis, route)


def amplitudes(left, right, left_energy, right_energy, virtual):
    coupling = lax.dot_general(
        left,
        right,
        (((1,), (1,)), ((), ())),
        precision=lax.Precision.HIGHEST,
        preferred_element_type=jnp.float32,
    )
    denom = left_energy + right_energy - virtual[:, None] - virtual[None, :]
    scaled = coupling / denom
    return 2.0 * scaled - scaled.T


def matmul(left, right):
    return jnp.dot(left, right, precision=lax.Precision.HIGHEST, preferred_element_type=jnp.float32)


def matmul_left_t(left, right):
    return lax.dot_general(
        left,
        right,
        (((0,), (0,)), ((), ())),
        precision=lax.Precision.HIGHEST,
        preferred_element_type=jnp.float32,
    )


def lookup(table, position):
    return jnp.sum(
        jnp.where(
            jnp.arange(table.shape[0], dtype=jnp.int32) == position, table, jnp.zeros_like(table)
        )
    )


def body(slices, occ_energy, virt_energy, order, near_keep, far_keep):
    cycle_size = lax.axis_size("orb")
    middle = cycle_size // 2
    position = lax.axis_index("orb")
    next_pos = (position + 1) % cycle_size
    far_pos = (position + middle) % cycle_size
    own_energy = lookup(occ_energy, lookup(order, position))
    next_energy = lookup(occ_energy, lookup(order, next_pos))
    far_energy = lookup(occ_energy, lookup(order, far_pos))
    near_weight = near_keep[0].astype(jnp.float32)
    far_weight = lookup(far_keep, position % middle).astype(jnp.float32)
    own = slices[0]
    nearby = passed_along(slices, "orb", -1)[0]
    near_amps = amplitudes(own, nearby, own_energy, next_energy, virt_energy) * near_weight
    partner = matmul_left_t(near_amps, own)
    returned = passed_along(partner, "orb", 1)
    diag_amps = amplitudes(own, own, own_energy, own_energy, virt_energy)
    density = matmul(diag_amps, own) + matmul(near_amps, nearby)
    facing = passed_along(slices, "orb", middle)[0]
    far_amps = amplitudes(own, facing, own_energy, far_energy, virt_energy) * far_weight
    density = density + matmul(far_amps, facing)
    density = density + returned
    return density[None]


def solution(mesh):
    return jax.shard_map(
        body,
        mesh=mesh,
        in_specs=(
            P(("frag", "orb"), None, None),
            P("frag"),
            P("frag"),
            P("frag"),
            P(("frag", "orb")),
            P("frag"),
        ),
        out_specs=P(("frag", "orb"), None, None),
        check_vma=False,
    )
```

profile of v0, /device:TPU:40, one launch (start us, length us, event | category | flops | bytes accessed | tf_op | source)
XLA Modules:
  0.0 355.9 jit_solution(3748376157707976215)
XLA Ops:
  0.0 24.5 %collective-permute-start = (f32[1,640,1024]{2,1,0:T(8,128)}, f32[1,640,1024]{2,1,0:T(8,128)S(1)}, u32[]{:S(2)}, u32[]{:S(2)}) collective-permute-start(f32[1,640,1024]{2,1,0:T(8,128)} %param.6), channel_id=1, source_target_pairs={{1,0},{2,1},{3,2},{4,3},{5,4},{6,5},{7,6},{8,7},{9,8},{10,9},{11,1... | collective-permute-start | bytes 7864328 | tf_op jit(solution)/shard_map/ppermute | solution.py:10
  24.5 0.0 collective-permute-start.1
  24.5 1.4 fusion.48
  25.9 3.2 fusion.49
  33.7 0.7 broadcast_subtract_fusion
  34.4 242.7 %collective-permute-done = f32[1,640,1024]{2,1,0:T(8,128)S(1)} collective-permute-done((f32[1,640,1024]{2,1,0:T(8,128)}, f32[1,640,1024]{2,1,0:T(8,128)S(1)}, u32[]{:S(2)}, u32[]{:S(2)}) %collective-permute-start) | collective-permute-done | bytes 2621472 | tf_op jit(solution)/shard_map/ppermute | solution.py:10
  277.1 0.0 copy-start.3
  277.1 1.5 copy-done.3
  278.6 8.9 %fusion.6 = f32[640,640]{1,0:T(8,128)} fusion(f32[1,640,1024]{2,1,0:T(8,128)S(1)} %collective-permute-done, f32[1,640,1024]{2,1,0:T(8,128)} %param.6), kind=kOutput, calls=%fused_computation.6 | convolution fusion | flops 5033164800 | bytes 6881280 | tf_op jit(solution)/shard_map/dot_general | solution.py:14
  287.6 0.0 copy-start
  287.6 0.0 copy-start.6
  287.6 2.9 copy.8
  290.5 0.0 copy-done
  290.5 0.0 copy-done.6
  290.5 9.7 %fusion.8 = f32[640,1024]{1,0:T(8,128)} fusion(f32[1,640,1024]{2,1,0:T(8,128)S(1)} %copy-done, f32[640,640]{1,0:T(8,128)} %fusion.6, f32[640,640]{0,1:T(8,128)} %copy.8, f32[]{:T(128)} %bitcast.4, f32[640]{0:T(1024)S(1)} %get-tuple-element.13, f32[640]{0:T(1024)S(1)} %copy-done.6), kind=kOutput, calls=%fused_computation.8 | convolution fusion | flops 5036032000 | bytes 8524804 | tf_op jit(solution)/shard_map/dot_general | solution.py:31
  300.2 0.2 collective-permute-start.2
  300.4 7.6 %fusion.14 = f32[640,640]{1,0:T(8,128)} fusion(f32[1,640,1024]{2,1,0:T(8,128)S(1)} %copy-done), kind=kOutput, calls=%fused_computation.14 | convolution fusion | flops 5033164800 | bytes 4259840 | tf_op jit(solution)/shard_map/dot_general | solution.py:14
  308.0 0.0 copy-start.7
  308.0 2.9 copy.7
  311.0 0.0 copy-done.7
  311.0 0.7 fusion.50
  312.3 10.2 %fusion.12 = f32[640,1024]{1,0:T(8,128)} fusion(f32[1,640,1024]{2,1,0:T(8,128)S(1)} %copy-done, f32[640,640]{1,0:T(8,128)} %fusion.14, f32[640,640]{0,1:T(8,128)} %copy.7, f32[640]{0:T(1024)S(1)} %copy-done.6, f32[640]{0:T(1024)S(1)} %get-tuple-element.12), kind=kOutput, calls=%fused_computation.12 | convolution fusion | flops 5035622400 | bytes 8524800 | tf_op jit(solution)/shard_map/dot_general | solution.py:27
  322.5 0.0 collective-permute-done.1
  322.5 9.6 %fusion.2 = f32[640,640]{1,0:T(8,128)} fusion(f32[1,640,1024]{2,1,0:T(8,128)} %collective-permute-done.1, f32[1,640,1024]{2,1,0:T(8,128)S(1)} %copy-done), kind=kOutput, calls=%fused_computation.2 | convolution fusion | flops 5033164800 | bytes 6881280 | tf_op jit(solution)/shard_map/dot_general | solution.py:14
  332.1 0.0 copy-start.1
  332.1 0.0 copy-start.4
  332.1 2.9 copy.9
  335.0 0.0 copy-done.1
  335.0 0.0 copy-done.4
  335.0 0.0 copy-start.2
  335.0 0.0 copy-start.5
  335.0 0.0 copy-start.8
  335.1 8.9 %fusion.4 = f32[640,1024]{1,0:T(8,128)S(1)} fusion(f32[1,640,1024]{2,1,0:T(8,128)} %copy-done.3, f32[640,640]{1,0:T(8,128)S(1)} %copy-done.1, f32[640,640]{0,1:T(8,128)S(1)} %copy-done.4, f32[]{:T(128)} %bitcast.4, f32[640]{0:T(1024)S(1)} %get-tuple-element.13, f32[640]{0:T(1024)S(1)} %copy-done.6), kind=kOutput, calls=%fused_computation.4 | convolution fusion | flops 5036032000 | bytes 8524804 | tf_op jit(solution)/shard_map/dot_general | solution.py:27
  344.0 0.0 collective-permute-done.2
  344.0 0.0 copy-done.2
  344.0 0.0 copy-done.5
  344.0 0.0 copy-done.8
  344.0 11.3 %add_bitcast_fusion = f32[1,640,1024]{2,1,0:T(8,128)} fusion(f32[640,1024]{1,0:T(8,128)} %collective-permute-done.2, f32[640,1024]{1,0:T(8,128)S(1)} %copy-done.8, f32[640,1024]{1,0:T(8,128)S(1)} %fusion.4, f32[1,640,1024]{2,1,0:T(8,128)} %collective-permute-done.1, f32[640,640]{1,0:T(8,128)S(1)} %copy-done.2, f32[640,640]{0,1:T(8,128)S(1)} %copy-done.5, ...), kind=kOutput, calls=%fused_computation.16 | convolution fusion | flops 5037998080 | bytes 16389124 | tf_op jit(solution)/shard_map/dot_general | solution.py:27
Async XLA Ops:
  0.0 277.1 %collective-permute-start = (f32[1,640,1024]{2,1,0:T(8,128)}, f32[1,640,1024]{2,1,0:T(8,128)S(1)}, u32[]{:S(2)}, u32[]{:S(2)}) collective-permute-start(f32[1,640,1024]{2,1,0:T(8,128)} %param.6), channel_id=1, source_target_pairs={{1,0},{2,1},{3,2},{4,3},{5,4},{6,5},{7,6},{8,7},{9,8},{10,9},{11,1... | collective-permute-start | bytes 7864328 | tf_op jit(solution)/shard_map/ppermute | solution.py:10
  24.5 298.0 %collective-permute-start.1 = (f32[1,640,1024]{2,1,0:T(8,128)}, f32[1,640,1024]{2,1,0:T(8,128)}, u32[]{:S(2)}, u32[]{:S(2)}) collective-permute-start(f32[1,640,1024]{2,1,0:T(8,128)} %param.6), channel_id=1, source_target_pairs={{64,0},{65,1},{66,2},{67,3},{68,4},{69,5},{70,6},{71,7},{72,8},{73... | collective-permute-start | bytes 7864328 | tf_op jit(solution)/shard_map/ppermute | solution.py:10
  277.1 1.5 copy-start.3
  287.6 2.9 copy-start
  287.6 2.9 copy-start.6
  300.2 43.8 %collective-permute-start.2 = (f32[640,1024]{1,0:T(8,128)}, f32[640,1024]{1,0:T(8,128)}, u32[]{:S(2)}, u32[]{:S(2)}) collective-permute-start(f32[640,1024]{1,0:T(8,128)} %fusion.8), channel_id=1, source_target_pairs={{127,0},{0,1},{1,2},{2,3},{3,4},{4,5},{5,6},{6,7},{7,8},{8,9},{9,1... | collective-permute-start | bytes 7864328 | tf_op jit(solution)/shard_map/ppermute | solution.py:10
  308.0 3.0 copy-start.7
  332.1 2.9 copy-start.1
  332.1 2.9 copy-start.4
  335.0 9.0 %copy-start.2 = (f32[640,640]{1,0:T(8,128)S(1)}, f32[640,640]{1,0:T(8,128)}, u32[]{:S(2)}) copy-start(f32[640,640]{1,0:T(8,128)} %fusion.2) | copy-start | bytes 4915204
  335.0 9.0 %copy-start.5 = (f32[640,640]{0,1:T(8,128)S(1)}, f32[640,640]{0,1:T(8,128)}, u32[]{:S(2)}) copy-start(f32[640,640]{0,1:T(8,128)} %copy.9) | copy-start | bytes 4915204
  335.0 9.0 %copy-start.8 = (f32[640,1024]{1,0:T(8,128)S(1)}, f32[640,1024]{1,0:T(8,128)}, u32[]{:S(2)}) copy-start(f32[640,1024]{1,0:T(8,128)} %fusion.12) | copy-start | bytes 7864324
where the time goes:
time: 363 us; the launch traced here: 356 us
  waiting for transfers between devices  243 us (67%)
  matrix products  66.3 us (18%)
  starting transfers between devices  24.7 us (7%)
  local copies, waits for them, and re-layouts  10.3 us (3%)
  other arithmetic  6.01 us (2%)
  between operations  5.82 us (2%)
    ppermute x3, waiting for transfers between devices, passed_along(): return lax.ppermute(block, axis, route)  243 us
    dot_general x3, matrix products, matmul(): jnp.dot(left, right, precision=lax.Precision.HIGHEST, preferred_element_t...  30.5 us
    dot_general x3, matrix products, amplitudes(): lax.dot_general(left, right, (((1,), (1,)), ((), ())), precision=lax.Prec...  26.1 us
    ppermute x3, starting transfers between devices, passed_along(): return lax.ppermute(block, axis, route)  24.7 us
    dot_general x1, matrix products, matmul_left_t(): lax.dot_general(left, right, (((0,), (0,)), ((), ())), precision=lax.Prec...  9.71 us
    dot_general x3, local copies, waits for them, and re-layouts, amplitudes(): lax.dot_general(left, right, (((1,), (1,)), ((), ())), precision=lax.Prec...  8.76 us
  transfers between devices with their start and end apart: 3, of which 1 were waited for; matrix products, arithmetic and copies ran while one was open for 20% of the time, Pallas kernels for 0%

commit v1 on v0

v1 whole, which is shorter than its diff:
```python
import functools

import jax
import jax.numpy as jnp
from jax import lax
from jax.experimental import pallas as pl
from jax.experimental.pallas import tpu as pltpu
from jax.sharding import PartitionSpec as P

MESH = pl.DeviceIdType.MESH
ROW = 8
CORES = 2
COLS = ROW // CORES
OWN, NEXT, PREV, FAR = range(4)
STEP = 128
TILE = 256
F32 = jnp.float32
BF16 = jnp.bfloat16


def split(x):
    high = x.astype(BF16)
    return high, (x - high.astype(F32)).astype(BF16)


def nt(left, right):
    return lax.dot_general(left, right, (((1,), (1,)), ((), ())), preferred_element_type=F32)


def nn(left, right):
    return jnp.dot(left, right, preferred_element_type=F32)


def kernel(
    n,
    own_ref, occ_ref, virt_ref, order_ref, near_ref, far_ref,
    out_ref,
    transit, held, relay, own_high, own_low, high, low, amp, virt_col, virt_row, weight,
    send_sem, recv_sem, near_send, near_recv, relay_send, relay_recv, weight_sem, load_sem, ready_sem,
):
    rows, depth = out_ref.shape
    rounds = rows // STEP
    half = STEP // 2
    middle = n // 2
    hops = middle // ROW
    quarter = rows // COLS
    me = lax.axis_index("orb")
    inside = lax.rem(me, ROW)
    base = me - inside
    core = lax.rem(inside, CORES)
    col = inside // CORES
    above = lax.rem(me + ROW, n)
    below = lax.rem(me + n - ROW, n)
    after = lax.rem(me + 1, n)
    before = lax.rem(me + n - 1, n)
    opposite = lax.rem(me + middle, n)
    first = inside == 0
    last = inside == ROW - 1

    barrier = pltpu.get_barrier_semaphore()

    def greet(device):
        pl.semaphore_signal(barrier, inc=1, device_id={"orb": device}, device_id_type=MESH)

    load = pltpu.make_async_copy(own_ref, held.at[OWN], load_sem)
    load.start()
    for shift in range(1, ROW):
        greet(base + lax.rem(inside + shift, ROW))
    greet(below)

    @pl.when(first)
    def _():
        greet(before)

    pl.semaphore_wait(barrier, jnp.where(last, ROW + 1, ROW))
    pl.semaphore_signal(ready_sem, inc=1, device_id={"orb": above}, device_id_type=MESH)
    load.wait()
    own = held.at[OWN]

    def remote(src, dst, send, recv, device):
        return pltpu.make_async_remote_copy(
            src_ref=src, dst_ref=dst, send_sem=send, recv_sem=recv,
            device_id={"orb": device}, device_id_type=MESH,
        )

    def lane(part, way):
        return pl.ds(pl.multiple_of(part * STEP + way * half, half), half)

    def start_hop(slot, way):
        hop, part = slot // rounds, lax.rem(slot, rounds)
        target = (above, below)[way]
        at = lane(part, way)
        sems = send_sem.at[slot, way], recv_sem.at[slot, way]

        @pl.when(hop == 0)
        def _():
            remote(own.at[at], transit.at[0, at], *sems, target).start()

        @pl.when((hop > 0) & (hop < hops - 1))
        def _():
            remote(transit.at[hop - 1, at], transit.at[hop, at], *sems, target).start()

        @pl.when(hop == hops - 1)
        def _():
            remote(transit.at[hop - 1, at], held.at[FAR, at], *sems, target).start()

    def far_copy(slot, way):
        at = pl.ds(way * half, half)
        return remote(own.at[at], transit.at[0, at], send_sem.at[slot, way], recv_sem.at[slot, way], above)

    def crossing(src, device):
        return remote(src, relay.at[1], relay_send.at[COLS], relay_recv.at[1], device)

    def to_relay(q, device):
        at = pl.ds(q * quarter, quarter)
        return remote(own.at[at], relay.at[0], relay_send.at[q], relay_recv.at[0], device)

    def near_copy(q, slot, device):
        at = pl.ds(q * quarter, quarter)
        return remote(own.at[at], held.at[slot, at], near_send.at[slot, q], near_recv.at[slot, q], device)

    def weight_copy():
        return remote(weight.at[NEXT], weight.at[PREV], weight_sem.at[0], weight_sem.at[1], after)

    def deliver(slot, device):
        at = pl.ds(pl.multiple_of(col * quarter, quarter), quarter)
        return remote(relay.at[1], held.at[slot, at], relay_send.at[COLS + 1], near_recv.at[slot, col], device)

    @pl.when(last)
    def _():
        crossing(own.at[pl.ds(rows - quarter, quarter)], above).start()
        for q in range(COLS - 1):
            to_relay(q, base + q * CORES + 1).start()

    @pl.when(first)
    def _():
        for q in range(1, COLS):
            to_relay(q, base + q * CORES).start()

    def send_first(way):
        def one(slot, carry):
            start_hop(slot, way)
            return carry

        lax.fori_loop(0, rounds, one, 0)

    send_first(0)

    @pl.when(~last)
    def _():
        for q in range(COLS):
            near_copy(q, PREV, after).start()

    @pl.when(~first)
    def _():
        for q in range(COLS):
            near_copy(q, NEXT, before).start()

    pl.semaphore_wait(ready_sem, 1)

    @pl.when(first)
    def _():
        crossing(own.at[pl.ds(0, quarter)], below).start()

    send_first(1)

    weight[OWN] = jnp.ones(weight.shape[1:], F32)
    weight[NEXT] = jnp.full(weight.shape[1:], near_ref[0].astype(F32), F32)
    weight[FAR] = jnp.full(weight.shape[1:], far_ref[lax.rem(me, middle)].astype(F32), F32)
    virt_row[...] = virt_ref[...].reshape(1, rows)
    virt_col[...] = jnp.broadcast_to(virt_row[...], (STEP, rows)).T

    def prepare(part, carry):
        at = pl.ds(pl.multiple_of(part * STEP, STEP), STEP)
        own_high[at], own_low[at] = split(held[OWN, at])
        high[at] = jnp.zeros((STEP, depth), BF16)
        low[at] = jnp.zeros((STEP, depth), BF16)
        out_ref[at] = jnp.zeros((STEP, depth), F32)
        return carry

    lax.fori_loop(0, rounds, prepare, 0)

    def energy(position):
        return occ_ref[order_ref[position]]

    def compute(which, part):
        at = pl.ds(pl.multiple_of(part * STEP, STEP), STEP)
        partner = jnp.where(which == OWN, me, jnp.where(which == NEXT, after, jnp.where(which == PREV, before, opposite)))
        total = energy(me) + energy(partner)
        w = weight[which, 0:1]
        new_high, new_low = split(held[which, at])
        high[at], low[at] = new_high, new_low
        both = jnp.concatenate([new_high, new_low], axis=0)
        wide = nt(own_high[...], both)
        coupling = wide[:, :STEP] + wide[:, STEP:] + nt(own_low[...], new_high)
        mine = coupling / (total - virt_col[...] - virt_row[:, at])
        amp[:, at] = mine
        row = lax.broadcasted_iota(jnp.int32, (rows, STEP), 0)
        theirs = jnp.where(row < (part + 1) * STEP, amp[at].T, 0.0)
        tilde_high, tilde_low = split(w * (2.0 * mine - theirs))
        tilde_twice = jnp.concatenate([tilde_high, tilde_high], axis=1)
        turned_high, turned_low = split((w * jnp.where(row < part * STEP, mine, 0.0)).T)
        turned = jnp.concatenate([turned_high, turned_low], axis=0)

        def columns(tile, carry):
            over = pl.ds(pl.multiple_of(tile * TILE, TILE), TILE)
            near_high, near_low = high[at, over], low[at, over]
            out_ref[:, over] += nn(tilde_twice, jnp.concatenate([near_high, near_low], axis=0)) + nn(tilde_low, near_high)
            back = nn(turned, high[:, over])
            out_ref[at, over] -= back[:STEP] + back[STEP:] + nn(turned_high, low[:, over])
            return carry

        lax.fori_loop(0, depth // TILE, columns, 0)

    slots = hops * rounds
    own_from, near_from = 3, 18
    near_to = near_from + 2 * rounds

    def step(slot, carry):
        far_copy(slot, 0).wait_recv()
        far_copy(slot, 1).wait_recv()

        @pl.when(slot + rounds < slots)
        def _():
            start_hop(slot + rounds, 0)
            start_hop(slot + rounds, 1)

        @pl.when(slot == 1)
        def _():
            weight_copy().start()

        @pl.when((slot == 2) & ~(first | last))
        def _():
            to_relay(0, above).wait_recv()

            @pl.when(core == 1)
            def _():
                crossing(relay.at[0], above).start()

            @pl.when(core == 0)
            def _():
                crossing(relay.at[0], below).start()

        @pl.when(slot == 9)
        def _():
            crossing(relay.at[0], above).wait_recv()

            @pl.when(core == 1)
            def _():
                deliver(PREV, base).start()

            @pl.when(core == 0)
            def _():
                deliver(NEXT, base + ROW - 1).start()

        @pl.when(slot == near_from)
        def _():
            for q in range(COLS):
                near_copy(q, NEXT, before).wait_recv()

        @pl.when(slot == near_from + rounds)
        def _():
            weight_copy().wait_recv()
            for q in range(COLS):
                near_copy(q, PREV, after).wait_recv()

        early = slot < own_from + rounds
        late = slot >= slots - rounds
        since = slot - near_from

        @pl.when((early & (slot >= own_from)) | ((since >= 0) & (slot < near_to)) | late)
        def _():
            which = jnp.where(early, OWN, jnp.where(late, FAR, NEXT + since // rounds))
            part = jnp.where(early, slot - own_from, jnp.where(late, slot - (slots - rounds), lax.rem(since, rounds)))
            compute(which, part)

        return carry

    lax.fori_loop(0, slots, step, 0)

    def sent(slot, carry):
        far_copy(slot, 0).wait_send()
        far_copy(slot, 1).wait_send()
        return carry

    lax.fori_loop(0, slots, sent, 0)
    weight_copy().wait_send()
    crossing(relay.at[0], above).wait_send()
    deliver(PREV, base).wait_send()

    @pl.when(last)
    def _():
        for q in range(COLS - 1):
            to_relay(q, above).wait_send()

    @pl.when(first)
    def _():
        for q in range(1, COLS):
            to_relay(q, above).wait_send()

    @pl.when(~last)
    def _():
        for q in range(COLS):
            near_copy(q, PREV, after).wait_send()

    @pl.when(~first)
    def _():
        for q in range(COLS):
            near_copy(q, NEXT, before).wait_send()


def body(slices, occ_energy, virt_energy, order, near_keep, far_keep):
    n = lax.axis_size("orb")
    rows, depth = slices.shape[1:]
    hops = n // 2 // ROW
    rounds = rows // STEP
    quarter = rows // COLS
    vmem = pl.BlockSpec(memory_space=pltpu.VMEM)
    smem = pl.BlockSpec(memory_space=pltpu.SMEM)
    dma = pltpu.SemaphoreType.DMA
    density = pl.pallas_call(
        functools.partial(kernel, n),
        out_shape=jax.ShapeDtypeStruct((rows, depth), F32),
        in_specs=[pl.BlockSpec(memory_space=pl.ANY), smem, vmem, smem, smem, smem],
        out_specs=vmem,
        scratch_shapes=[
            pltpu.VMEM((hops - 1, rows, depth), F32),
            pltpu.VMEM((4, rows, depth), F32),
            pltpu.VMEM((2, quarter, depth), F32),
            pltpu.VMEM((rows, depth), BF16),
            pltpu.VMEM((rows, depth), BF16),
            pltpu.VMEM((rows, depth), BF16),
            pltpu.VMEM((rows, depth), BF16),
            pltpu.VMEM((rows, rows), F32),
            pltpu.VMEM((rows, STEP), F32),
            pltpu.VMEM((1, rows), F32),
            pltpu.VMEM((4, 8, STEP), F32),
            dma((hops * rounds, 2)),
            dma((hops * rounds, 2)),
            dma((4, COLS)),
            dma((4, COLS)),
            dma((COLS + 2,)),
            dma((2,)),
            dma((2,)),
            dma,
            pltpu.SemaphoreType.REGULAR,
        ],
        compiler_params=pltpu.CompilerParams(
            collective_id=0, has_side_effects=True, vmem_limit_bytes=62 * 1024 * 1024
        ),
    )(slices[0], occ_energy, virt_energy, order, near_keep, far_keep)
    return density[None]


def solution(mesh):
    return jax.shard_map(
        body,
        mesh=mesh,
        in_specs=(
            P(("frag", "orb"), None, None),
            P("frag"),
            P("frag"),
            P("frag"),
            P(("frag", "orb")),
            P("frag"),
        ),
        out_specs=P(("frag", "orb"), None, None),
        check_vma=False,
    )
```

time: 363 us -> 272 us (0.75)
  the two profiles are of different devices: /device:TPU:40 before, /device:TPU:33 now
where the time goes in v1:
time: 272 us
  Pallas kernels  268 us (99%)
  local copies, waits for them, and re-layouts  3.56 us (1%)
    pallas_call x1, Pallas kernels, body(): pl.pallas_call(functools.partial(kernel, n), out_shape=jax.ShapeDtypeStru...  268 us

profile of v1, /device:TPU:33, one launch (start us, length us, event | category | flops | bytes accessed | tf_op | source)
XLA Modules:
  0.0 272.0 jit_solution(18102520570248269792)
XLA Ops:
  0.7 267.7 %shard_map.64 = f32[640,1024]{1,0:T(8,128)} custom-call(f32[640,1024]{1,0:T(8,128)} %bitcast.3, f32[128]{0:T(128)} %occ_ref.1, f32[640]{0:T(1024)} %virt_ref.1, s32[128]{0:T(128)} %order_ref.1, s32[1]{0:T(128)S(6)} %copy.8.near_ref, s32[64]{0:T(128)} %far_ref.1), custom_call_target="tpu_custom_call" | custom-call | tf_op jit(solution)/shard_map/pallas_call | solution.py:321
  268.4 3.6 %copy.9 = f32[1,640,1024]{2,1,0:T(8,128)} copy(f32[1,640,1024]{2,1,0:T(8,128)} %bitcast.2) | data formatting | bytes 5242880

commit v2 on v1

--- a/solution.py
+++ b/solution.py
@@ -14,6 +14,8 @@
 OWN, NEXT, PREV, FAR = range(4)
 STEP = 128
 TILE = 256
+MOVED = 2
+SHIFT = 8
 F32 = jnp.float32
 BF16 = jnp.bfloat16
 
@@ -35,7 +37,7 @@
     n,
     own_ref, occ_ref, virt_ref, order_ref, near_ref, far_ref,
     out_ref,
-    transit, held, relay, own_high, own_low, high, low, amp, virt_col, virt_row, weight,
+    transit_up, transit_down, held, relay, own_high, own_low, high, low, amp, virt_col, virt_row, weight,
     send_sem, recv_sem, near_send, near_recv, relay_send, relay_recv, weight_sem, load_sem, ready_sem,
 ):
     rows, depth = out_ref.shape
@@ -47,6 +49,8 @@
     me = lax.axis_index("orb")
     inside = lax.rem(me, ROW)
     base = me - inside
+    ring = n // ROW
+    place = me // ROW
     core = lax.rem(inside, CORES)
     col = inside // CORES
     above = lax.rem(me + ROW, n)
@@ -83,30 +87,53 @@
             device_id={"orb": device}, device_id_type=MESH,
         )
 
-    def lane(part, way):
-        return pl.ds(pl.multiple_of(part * STEP + way * half, half), half)
+    def on_chunk(slot, way, source, act):
+        part = lax.rem(slot, rounds)
+        moved = (source >= hops) & (part < MOVED)
+        for shift in (0, SHIFT):
+            size = half - shift if way == 0 else half + shift
+            offset = 0 if way == 0 else half - shift
+            at = pl.ds(pl.multiple_of(part * STEP + offset, SHIFT), size)
+            within = pl.ds(pl.multiple_of(part * (half + way * SHIFT), SHIFT), size)
+
+            @pl.when(moved if shift else ~moved)
+            def _():
+                act(at, within)
+
+    def source_of(hop, way):
+        return lax.rem(place + (ring - hop if way == 0 else hop), ring)
 
     def start_hop(slot, way):
-        hop, part = slot // rounds, lax.rem(slot, rounds)
+        hop = slot // rounds
         target = (above, below)[way]
-        at = lane(part, way)
         sems = send_sem.at[slot, way], recv_sem.at[slot, way]
 
-        @pl.when(hop == 0)
-        def _():
-            remote(own.at[at], transit.at[0, at], *sems, target).start()
-
-        @pl.when((hop > 0) & (hop < hops - 1))
-        def _():
-            remote(transit.at[hop - 1, at], transit.at[hop, at], *sems, target).start()
-
-        @pl.when(hop == hops - 1)
-        def _():
-            remote(transit.at[hop - 1, at], held.at[FAR, at], *sems, target).start()
-
-    def far_copy(slot, way):
-        at = pl.ds(way * half, half)
-        return remote(own.at[at], transit.at[0, at], send_sem.at[slot, way], recv_sem.at[slot, way], above)
+        transit = (transit_up, transit_down)[way]
+
+        def act(at, within):
+            @pl.when(hop == 0)
+            def _():
+                remote(own.at[at], transit.at[0, within], *sems, target).start()
+
+            @pl.when((hop > 0) & (hop < hops - 1))
+            def _():
+                remote(transit.at[hop - 1, within], transit.at[hop, within], *sems, target).start()
+
+            @pl.when(hop == hops - 1)
+            def _():
+                remote(transit.at[hop - 1, within], held.at[FAR, at], *sems, target).start()
+
+        on_chunk(slot, way, source_of(hop, way), act)
+
+    def far_copy(slot, way, at):
+        sems = send_sem.at[slot, way], recv_sem.at[slot, way]
+        return remote(own.at[at], held.at[FAR, at], *sems, above)
+
+    def far_arrived(slot, way):
+        on_chunk(slot, way, source_of(slot // rounds + 1, way), lambda at, within: far_copy(slot, way, at).wait_recv())
+
+    def far_sent(slot, way):
+        on_chunk(slot, way, source_of(slot // rounds, way), lambda at, within: far_copy(slot, way, at).wait_send())
 
     def crossing(src, device):
         return remote(src, relay.at[1], relay_send.at[COLS], relay_recv.at[1], device)
@@ -213,35 +240,18 @@
         lax.fori_loop(0, depth // TILE, columns, 0)
 
     slots = hops * rounds
-    own_from, near_from = 3, 18
+    own_from, deliver_at, near_from = 3, 14, 22
     near_to = near_from + 2 * rounds
 
     def step(slot, carry):
-        far_copy(slot, 0).wait_recv()
-        far_copy(slot, 1).wait_recv()
-
-        @pl.when(slot + rounds < slots)
-        def _():
-            start_hop(slot + rounds, 0)
-            start_hop(slot + rounds, 1)
-
-        @pl.when(slot == 1)
-        def _():
-            weight_copy().start()
-
-        @pl.when((slot == 2) & ~(first | last))
-        def _():
-            to_relay(0, above).wait_recv()
-
-            @pl.when(core == 1)
-            def _():
-                crossing(relay.at[0], above).start()
-
-            @pl.when(core == 0)
-            def _():
-                crossing(relay.at[0], below).start()
-
-        @pl.when(slot == 9)
+        for way in range(2):
+            far_arrived(slot, way)
+
+            @pl.when(slot + rounds < slots)
+            def _():
+                start_hop(slot + rounds, way)
+
+        @pl.when(slot == deliver_at)
         def _():
             crossing(relay.at[0], above).wait_recv()
 
@@ -276,11 +286,25 @@
 
         return carry
 
+    weight_copy().start()
+
+    @pl.when(~(first | last))
+    def _():
+        to_relay(0, above).wait_recv()
+
+        @pl.when(core == 1)
+        def _():
+            crossing(relay.at[0], above).start()
+
+        @pl.when(core == 0)
+        def _():
+            crossing(relay.at[0], below).start()
+
     lax.fori_loop(0, slots, step, 0)
 
     def sent(slot, carry):
-        far_copy(slot, 0).wait_send()
-        far_copy(slot, 1).wait_send()
+        far_sent(slot, 0)
+        far_sent(slot, 1)
         return carry
 
     lax.fori_loop(0, slots, sent, 0)
@@ -324,7 +348,8 @@
         in_specs=[pl.BlockSpec(memory_space=pl.ANY), smem, vmem, smem, smem, smem],
         out_specs=vmem,
         scratch_shapes=[
-            pltpu.VMEM((hops - 1, rows, depth), F32),
+            pltpu.VMEM((hops - 1, rows // 2, depth), F32),
+            pltpu.VMEM((hops - 1, rows // 2 + rounds * SHIFT, depth), F32),
             pltpu.VMEM((4, rows, depth), F32),
             pltpu.VMEM((2, quarter, depth), F32),
             pltpu.VMEM((rows, depth), BF16),

time: 272 us -> 269 us (0.989)
  the two profiles are of different devices: /device:TPU:33 before, /device:TPU:34 now
where the time goes in v2:
time: 269 us
  Pallas kernels  265 us (99%)
  local copies, waits for them, and re-layouts  3.56 us (1%)
    pallas_call x1, Pallas kernels, body(): pl.pallas_call(functools.partial(kernel, n), out_shape=jax.ShapeDtypeStru...  265 us

profile of v2, /device:TPU:34, one launch (start us, length us, event | category | flops | bytes accessed | tf_op | source)
XLA Modules:
  0.0 268.9 jit_solution(5488016263929351140)
XLA Ops:
  0.7 264.7 %shard_map.64 = f32[640,1024]{1,0:T(8,128)} custom-call(f32[640,1024]{1,0:T(8,128)} %bitcast.3, f32[128]{0:T(128)} %occ_ref.1, f32[640]{0:T(1024)} %virt_ref.1, s32[128]{0:T(128)} %order_ref.1, s32[1]{0:T(128)S(6)} %copy.8.near_ref, s32[64]{0:T(128)} %far_ref.1), custom_call_target="tpu_custom_call" | custom-call | tf_op jit(solution)/shard_map/pallas_call | solution.py:345
  265.3 3.6 %copy.9 = f32[1,640,1024]{2,1,0:T(8,128)} copy(f32[1,640,1024]{2,1,0:T(8,128)} %bitcast.2) | data formatting | bytes 5242880

commit v3 on v1

v3 whole, which is shorter than its diff:
```python
import functools

import jax
import jax.numpy as jnp
from jax import lax
from jax.experimental import pallas as pl
from jax.experimental.pallas import tpu as pltpu
from jax.sharding import PartitionSpec as P

MESH = pl.DeviceIdType.MESH
ROW = 8
CORES = 2
OWN, NEXT, PREV, FAR = range(4)
STEP = 128
TILE = 256
F32 = jnp.float32
BF16 = jnp.bfloat16


def split(x):
    high = x.astype(BF16)
    return high, (x - high.astype(F32)).astype(BF16)


def nt(left, right):
    return lax.dot_general(left, right, (((1,), (1,)), ((), ())), preferred_element_type=F32)


def nn(left, right):
    return jnp.dot(left, right, preferred_element_type=F32)


def kernel(
    n,
    own_ref, occ_ref, virt_ref, order_ref, near_ref, far_ref,
    out_ref,
    transit, held, own_high, own_low, high, low, amp, virt_col, virt_row, weight,
    send_sem, recv_sem, near_send, near_recv, pass_send, weight_sem, load_sem,
):
    rows, depth = out_ref.shape
    rounds = rows // STEP
    middle = n // 2
    hops = middle // ROW
    slots = hops * rounds
    me = lax.axis_index("orb")
    inside = lax.rem(me, ROW)
    base = me - inside
    upward = lax.rem(inside, CORES) == 1
    above = lax.rem(me + ROW, n)
    below = lax.rem(me + n - ROW, n)
    onward = jnp.where(upward, above, below)
    after = lax.rem(me + 1, n)
    before = lax.rem(me + n - 1, n)
    opposite = lax.rem(me + middle, n)
    first = inside == 0
    last = inside == ROW - 1
    row_first, row_last = base, base + ROW - 1

    load = pltpu.make_async_copy(own_ref, held.at[OWN], load_sem)
    load.start()
    barrier = pltpu.get_barrier_semaphore()

    def greet(device):
        pl.semaphore_signal(barrier, inc=1, device_id={"orb": device}, device_id_type=MESH)

    greet(jnp.where(upward, below, above))
    greet(before)
    greet(jnp.where(last, row_first, after))

    @pl.when(first)
    def _():
        greet(row_last)

    pl.semaphore_wait(barrier, jnp.where(last, 4, 3))
    load.wait()
    own = held.at[OWN]

    def remote(src, dst, send, recv, device):
        return pltpu.make_async_remote_copy(
            src_ref=src, dst_ref=dst, send_sem=send, recv_sem=recv,
            device_id={"orb": device}, device_id_type=MESH,
        )

    def band(part):
        return pl.ds(pl.multiple_of(part * STEP, STEP), STEP)

    def start_hop(slot):
        hop, at = slot // rounds, band(lax.rem(slot, rounds))
        sems = send_sem.at[slot], recv_sem.at[slot]

        @pl.when(hop == 0)
        def _():
            remote(own.at[at], transit.at[0, at], *sems, onward).start()

        @pl.when((hop > 0) & (hop < hops - 1))
        def _():
            remote(transit.at[hop - 1, at], transit.at[hop, at], *sems, onward).start()

        @pl.when(hop == hops - 1)
        def _():
            remote(transit.at[hop - 1, at], held.at[FAR, at], *sems, onward).start()

    def far_copy(slot):
        at = pl.ds(0, STEP)
        return remote(own.at[at], transit.at[0, at], send_sem.at[slot], recv_sem.at[slot], onward)

    def near_copy(part, slot, device):
        at = band(part)
        return remote(own.at[at], held.at[slot, at], near_send.at[slot, part], near_recv.at[slot, part], device)

    def pass_copy(part, slot, device):
        at = band(part)
        return remote(transit.at[0, at], held.at[slot, at], pass_send.at[part], near_recv.at[slot, part], device)

    def weight_copy():
        return remote(weight.at[NEXT], weight.at[PREV], weight_sem.at[0], weight_sem.at[1], after)

    def over_parts(act):
        def one(part, carry):
            act(part)
            return carry

        lax.fori_loop(0, rounds, one, 0)

    over_parts(start_hop)

    @pl.when(~last)
    def _():
        over_parts(lambda part: near_copy(part, PREV, after).start())

    @pl.when(~first)
    def _():
        over_parts(lambda part: near_copy(part, NEXT, before).start())

    weight[OWN] = jnp.ones(weight.shape[1:], F32)
    weight[NEXT] = jnp.full(weight.shape[1:], near_ref[0].astype(F32), F32)
    weight[FAR] = jnp.full(weight.shape[1:], far_ref[lax.rem(me, middle)].astype(F32), F32)
    virt_row[...] = virt_ref[...].reshape(1, rows)
    virt_col[...] = jnp.broadcast_to(virt_row[...], (STEP, rows)).T

    def prepare(part, carry):
        at = pl.ds(pl.multiple_of(part * STEP, STEP), STEP)
        own_high[at], own_low[at] = split(held[OWN, at])
        high[at] = jnp.zeros((STEP, depth), BF16)
        low[at] = jnp.zeros((STEP, depth), BF16)
        out_ref[at] = jnp.zeros((STEP, depth), F32)
        return carry

    lax.fori_loop(0, rounds, prepare, 0)

    def energy(position):
        return occ_ref[order_ref[position]]

    def compute(which, part):
        at = pl.ds(pl.multiple_of(part * STEP, STEP), STEP)
        partner = jnp.where(which == OWN, me, jnp.where(which == NEXT, after, jnp.where(which == PREV, before, opposite)))
        total = energy(me) + energy(partner)
        w = weight[which, 0:1]
        new_high, new_low = split(held[which, at])
        high[at], low[at] = new_high, new_low
        both = jnp.concatenate([new_high, new_low], axis=0)
        wide = nt(own_high[...], both)
        coupling = wide[:, :STEP] + wide[:, STEP:] + nt(own_low[...], new_high)
        mine = coupling / (total - virt_col[...] - virt_row[:, at])
        amp[:, at] = mine
        row = lax.broadcasted_iota(jnp.int32, (rows, STEP), 0)
        theirs = jnp.where(row < (part + 1) * STEP, amp[at].T, 0.0)
        tilde_high, tilde_low = split(w * (2.0 * mine - theirs))
        tilde_twice = jnp.concatenate([tilde_high, tilde_high], axis=1)
        turned_high, turned_low = split((w * jnp.where(row < part * STEP, mine, 0.0)).T)
        turned = jnp.concatenate([turned_high, turned_low], axis=0)

        def columns(tile, carry):
            over = pl.ds(pl.multiple_of(tile * TILE, TILE), TILE)
            near_high, near_low = high[at, over], low[at, over]
            out_ref[:, over] += nn(tilde_twice, jnp.concatenate([near_high, near_low], axis=0)) + nn(tilde_low, near_high)
            back = nn(turned, high[:, over])
            out_ref[at, over] -= back[:STEP] + back[STEP:] + nn(turned_high, low[:, over])
            return carry

        lax.fori_loop(0, depth // TILE, columns, 0)

    own_from, near_from = 3, 20
    near_to = near_from + 2 * rounds

    def step(slot, carry):
        far_copy(slot).wait_recv()

        @pl.when(slot + rounds < slots)
        def _():
            start_hop(slot + rounds)

        @pl.when((slot < rounds) & last)
        def _():
            pass_copy(slot, PREV, row_first).start()

        @pl.when((slot < rounds) & first)
        def _():
            pass_copy(slot, NEXT, row_last).start()

        @pl.when(slot == near_from)
        def _():
            over_parts(lambda part: near_copy(part, NEXT, before).wait_recv())

        @pl.when(slot == near_from + rounds)
        def _():
            weight_copy().wait_recv()
            over_parts(lambda part: near_copy(part, PREV, after).wait_recv())

        early = slot < own_from + rounds
        late = slot >= slots - rounds
        since = slot - near_from

        @pl.when((early & (slot >= own_from)) | ((since >= 0) & (slot < near_to)) | late)
        def _():
            which = jnp.where(early, OWN, jnp.where(late, FAR, NEXT + since // rounds))
            part = jnp.where(early, slot - own_from, jnp.where(late, slot - (slots - rounds), lax.rem(since, rounds)))
            compute(which, part)

        return carry

    weight_copy().start()
    lax.fori_loop(0, slots, step, 0)

    def sent(slot, carry):
        far_copy(slot).wait_send()
        return carry

    lax.fori_loop(0, slots, sent, 0)
    weight_copy().wait_send()

    @pl.when(first | last)
    def _():
        over_parts(lambda part: pass_copy(part, PREV, after).wait_send())

    @pl.when(~last)
    def _():
        over_parts(lambda part: near_copy(part, PREV, after).wait_send())

    @pl.when(~first)
    def _():
        over_parts(lambda part: near_copy(part, NEXT, before).wait_send())


def body(slices, occ_energy, virt_energy, order, near_keep, far_keep):
    n = lax.axis_size("orb")
    rows, depth = slices.shape[1:]
    hops = n // 2 // ROW
    rounds = rows // STEP
    vmem = pl.BlockSpec(memory_space=pltpu.VMEM)
    smem = pl.BlockSpec(memory_space=pltpu.SMEM)
    dma = pltpu.SemaphoreType.DMA
    density = pl.pallas_call(
        functools.partial(kernel, n),
        out_shape=jax.ShapeDtypeStruct((rows, depth), F32),
        in_specs=[pl.BlockSpec(memory_space=pl.ANY), smem, vmem, smem, smem, smem],
        out_specs=vmem,
        scratch_shapes=[
            pltpu.VMEM((hops - 1, rows, depth), F32),
            pltpu.VMEM((4, rows, depth), F32),
            pltpu.VMEM((rows, depth), BF16),
            pltpu.VMEM((rows, depth), BF16),
            pltpu.VMEM((rows, depth), BF16),
            pltpu.VMEM((rows, depth), BF16),
            pltpu.VMEM((rows, rows), F32),
            pltpu.VMEM((rows, STEP), F32),
            pltpu.VMEM((1, rows), F32),
            pltpu.VMEM((4, 8, STEP), F32),
            dma((hops * rounds,)),
            dma((hops * rounds,)),
            dma((4, rounds)),
            dma((4, rounds)),
            dma((rounds,)),
            dma((2,)),
            dma,
        ],
        compiler_params=pltpu.CompilerParams(
            collective_id=0, has_side_effects=True, vmem_limit_bytes=62 * 1024 * 1024
        ),
    )(slices[0], occ_energy, virt_energy, order, near_keep, far_keep)
    return density[None]


def solution(mesh):
    return jax.shard_map(
        body,
        mesh=mesh,
        in_specs=(
            P(("frag", "orb"), None, None),
            P("frag"),
            P("frag"),
            P("frag"),
            P(("frag", "orb")),
            P("frag"),
        ),
        out_specs=P(("frag", "orb"), None, None),
        check_vma=False,
    )
```

time: 272 us -> 262 us (0.963)
  Pallas kernels: 268 us -> 258 us
    pallas_call x1, Pallas kernels: 268 us -> 258 us  [body(): pl.pallas_call(functools.partial(kernel, n), out_shape=jax.ShapeDtypeStru...]
where the time goes in v3:
time: 262 us
  Pallas kernels  258 us (98%)
  local copies, waits for them, and re-layouts  3.56 us (1%)
    pallas_call x1, Pallas kernels, body(): pl.pallas_call(functools.partial(kernel, n), out_shape=jax.ShapeDtypeStru...  258 us

profile of v3, /device:TPU:33, one launch (start us, length us, event | category | flops | bytes accessed | tf_op | source)
XLA Modules:
  0.0 261.7 jit_solution(6089010809209926439)
XLA Ops:
  0.7 257.5 %shard_map.64 = f32[640,1024]{1,0:T(8,128)} custom-call(f32[640,1024]{1,0:T(8,128)} %bitcast.3, f32[128]{0:T(128)} %occ_ref.1, f32[640]{0:T(1024)} %virt_ref.1, s32[128]{0:T(128)} %order_ref.1, s32[1]{0:T(128)S(6)} %copy.8.near_ref, s32[64]{0:T(128)} %far_ref.1), custom_call_target="tpu_custom_call" | custom-call | tf_op jit(solution)/shard_map/pallas_call | solution.py:253
  258.2 3.6 %copy.9 = f32[1,640,1024]{2,1,0:T(8,128)} copy(f32[1,640,1024]{2,1,0:T(8,128)} %bitcast.2) | data formatting | bytes 5242880

commit v4 on v3

--- a/solution.py
+++ b/solution.py
@@ -13,6 +13,7 @@
 OWN, NEXT, PREV, FAR = range(4)
 STEP = 128
 TILE = 256
+MINOR = 24
 F32 = jnp.float32
 BF16 = jnp.bfloat16
 
@@ -34,8 +35,8 @@
     n,
     own_ref, occ_ref, virt_ref, order_ref, near_ref, far_ref,
     out_ref,
-    transit, held, own_high, own_low, high, low, amp, virt_col, virt_row, weight,
-    send_sem, recv_sem, near_send, near_recv, pass_send, weight_sem, load_sem,
+    transit, minor, held, own_high, own_low, high, low, amp, virt_col, virt_row, weight,
+    send_sem, recv_sem, minor_send, minor_recv, near_send, near_recv, pass_send, weight_sem, load_sem,
 ):
     rows, depth = out_ref.shape
     rounds = rows // STEP
@@ -49,6 +50,9 @@
     above = lax.rem(me + ROW, n)
     below = lax.rem(me + n - ROW, n)
     onward = jnp.where(upward, above, below)
+    feeder = jnp.where(upward, below, above)
+    ring = n // ROW
+    place = me // ROW
     after = lax.rem(me + 1, n)
     before = lax.rem(me + n - 1, n)
     opposite = lax.rem(me + middle, n)
@@ -63,15 +67,18 @@
     def greet(device):
         pl.semaphore_signal(barrier, inc=1, device_id={"orb": device}, device_id_type=MESH)
 
-    greet(jnp.where(upward, below, above))
-    greet(before)
-    greet(jnp.where(last, row_first, after))
+    greet(feeder)
+
+    @pl.when(upward)
+    def _():
+        greet(before)
+        greet(jnp.where(last, row_first, after))
 
     @pl.when(first)
     def _():
-        greet(row_last)
-
-    pl.semaphore_wait(barrier, jnp.where(last, 4, 3))
+        greet(before)
+
+    pl.semaphore_wait(barrier, jnp.where(upward, jnp.where(last, 2, 1), 3))
     load.wait()
     own = held.at[OWN]
 
@@ -84,25 +91,82 @@
     def band(part):
         return pl.ds(pl.multiple_of(part * STEP, STEP), STEP)
 
+    def moved(source):
+        return (source >= hops) == upward
+
+    def from_feeder(distance):
+        return lax.rem(place + jnp.where(upward, ring - distance, distance), ring)
+
+    def to_feeder(distance):
+        return lax.rem(place + jnp.where(upward, distance, ring - distance), ring)
+
+    def on_chunk(hop, part, source, act):
+        short = (hop > 0) & (part == 0) & moved(source)
+
+        @pl.when(short)
+        def _():
+            act(pl.ds(MINOR, STEP - MINOR))
+
+        @pl.when(~short)
+        def _():
+            act(band(part))
+
     def start_hop(slot):
-        hop, at = slot // rounds, band(lax.rem(slot, rounds))
+        hop, part = slot // rounds, lax.rem(slot, rounds)
         sems = send_sem.at[slot], recv_sem.at[slot]
 
-        @pl.when(hop == 0)
-        def _():
-            remote(own.at[at], transit.at[0, at], *sems, onward).start()
-
-        @pl.when((hop > 0) & (hop < hops - 1))
-        def _():
-            remote(transit.at[hop - 1, at], transit.at[hop, at], *sems, onward).start()
-
-        @pl.when(hop == hops - 1)
-        def _():
-            remote(transit.at[hop - 1, at], held.at[FAR, at], *sems, onward).start()
-
-    def far_copy(slot):
-        at = pl.ds(0, STEP)
+        def act(at):
+            @pl.when(hop == 0)
+            def _():
+                remote(own.at[at], transit.at[0, at], *sems, onward).start()
+
+            @pl.when((hop > 0) & (hop < hops - 1))
+            def _():
+                remote(transit.at[hop - 1, at], transit.at[hop, at], *sems, onward).start()
+
+            @pl.when(hop == hops - 1)
+            def _():
+                remote(transit.at[hop - 1, at], held.at[FAR, at], *sems, onward).start()
+
+        on_chunk(hop, part, from_feeder(hop), act)
+
+    def far_copy(slot, at):
         return remote(own.at[at], transit.at[0, at], send_sem.at[slot], recv_sem.at[slot], onward)
+
+    def far_arrived(slot):
+        hop, part = slot // rounds, lax.rem(slot, rounds)
+        on_chunk(hop, part, from_feeder(hop + 1), lambda at: far_copy(slot, at).wait_recv())
+
+    def far_sent(slot):
+        hop, part = slot // rounds, lax.rem(slot, rounds)
+        on_chunk(hop, part, from_feeder(hop), lambda at: far_copy(slot, at).wait_send())
+
+    few = pl.ds(0, MINOR)
+
+    def minor_copy(hop, src, dst):
+        return remote(src, dst, minor_send.at[hop], minor_recv.at[hop], feeder)
+
+    def minor_any(hop):
+        return minor_copy(hop, own.at[few], held.at[FAR, few])
+
+    def minor_hop(hop):
+        @pl.when(moved(to_feeder(hop)))
+        def _():
+            @pl.when(hop == 0)
+            def _():
+                minor_copy(hop, own.at[few], minor.at[0]).start()
+
+            @pl.when(hop > 0)
+            def _():
+                minor_any(hop - 1).wait_recv()
+
+            @pl.when((hop > 0) & (hop < hops - 1))
+            def _():
+                minor_copy(hop, minor.at[hop - 1], minor.at[hop]).start()
+
+            @pl.when(hop == hops - 1)
+            def _():
+                minor_copy(hop, minor.at[hop - 1], held.at[FAR, few]).start()
 
     def near_copy(part, slot, device):
         at = band(part)
@@ -124,13 +188,13 @@
 
     over_parts(start_hop)
 
-    @pl.when(~last)
+    @pl.when(~upward)
     def _():
         over_parts(lambda part: near_copy(part, PREV, after).start())
 
-    @pl.when(~first)
-    def _():
-        over_parts(lambda part: near_copy(part, NEXT, before).start())
+        @pl.when(~first)
+        def _():
+            over_parts(lambda part: near_copy(part, NEXT, before).start())
 
     weight[OWN] = jnp.ones(weight.shape[1:], F32)
     weight[NEXT] = jnp.full(weight.shape[1:], near_ref[0].astype(F32), F32)
@@ -180,32 +244,55 @@
 
         lax.fori_loop(0, depth // TILE, columns, 0)
 
-    own_from, near_from = 3, 20
+    own_from, near_from = 3, 24
+    stride = rounds - 1
     near_to = near_from + 2 * rounds
 
     def step(slot, carry):
-        far_copy(slot).wait_recv()
+        far_arrived(slot)
 
         @pl.when(slot + rounds < slots)
         def _():
             start_hop(slot + rounds)
 
-        @pl.when((slot < rounds) & last)
-        def _():
-            pass_copy(slot, PREV, row_first).start()
+        @pl.when((lax.rem(slot, stride) == 1) & (slot < hops * stride))
+        def _():
+            minor_hop(slot // stride)
+
+        @pl.when((slot == slots - rounds) & moved(lax.rem(place + hops, ring)))
+        def _():
+            minor_any(hops - 1).wait_recv()
 
         @pl.when((slot < rounds) & first)
         def _():
             pass_copy(slot, NEXT, row_last).start()
 
-        @pl.when(slot == near_from)
+        @pl.when((slot == 6) & upward)
+        def _():
+            over_parts(lambda part: near_copy(part, PREV, after).wait_recv())
+            over_parts(lambda part: near_copy(part, NEXT, before).start())
+
+        @pl.when((slot == 14) & upward)
         def _():
             over_parts(lambda part: near_copy(part, NEXT, before).wait_recv())
+            weight_copy().start()
+
+            @pl.when(last)
+            def _():
+                over_parts(lambda part: pass_copy(part, PREV, row_first).start())
+
+            @pl.when(~last)
+            def _():
+                over_parts(lambda part: near_copy(part, PREV, after).start())
+
+        @pl.when((slot == near_from) & ~upward)
+        def _():
+            over_parts(lambda part: near_copy(part, NEXT, before).wait_recv())
+            over_parts(lambda part: near_copy(part, PREV, after).wait_recv())
 
         @pl.when(slot == near_from + rounds)
         def _():
             weight_copy().wait_recv()
-            over_parts(lambda part: near_copy(part, PREV, after).wait_recv())
 
         early = slot < own_from + rounds
         late = slot >= slots - rounds
@@ -219,14 +306,26 @@
 
         return carry
 
-    weight_copy().start()
+    @pl.when(~upward)
+    def _():
+        weight_copy().start()
+
     lax.fori_loop(0, slots, step, 0)
 
     def sent(slot, carry):
-        far_copy(slot).wait_send()
+        far_sent(slot)
         return carry
 
     lax.fori_loop(0, slots, sent, 0)
+
+    def minor_sent(hop, carry):
+        @pl.when(moved(to_feeder(hop)))
+        def _():
+            minor_any(hop).wait_send()
+
+        return carry
+
+    lax.fori_loop(0, hops, minor_sent, 0)
     weight_copy().wait_send()
 
     @pl.when(first | last)
@@ -257,6 +356,7 @@
         out_specs=vmem,
         scratch_shapes=[
             pltpu.VMEM((hops - 1, rows, depth), F32),
+            pltpu.VMEM((hops - 1, MINOR, depth), F32),
             pltpu.VMEM((4, rows, depth), F32),
             pltpu.VMEM((rows, depth), BF16),
             pltpu.VMEM((rows, depth), BF16),
@@ -268,6 +368,8 @@
             pltpu.VMEM((4, 8, STEP), F32),
             dma((hops * rounds,)),
             dma((hops * rounds,)),
+            dma((hops,)),
+            dma((hops,)),
             dma((4, rounds)),
             dma((4, rounds)),
             dma((rounds,)),

time: 262 us -> 255 us (0.973)
  Pallas kernels: 258 us -> 251 us
    pallas_call x1, Pallas kernels: 258 us -> 251 us  [body(): pl.pallas_call(functools.partial(kernel, n), out_shape=jax.ShapeDtypeStru...]
where the time goes in v4:
time: 255 us
  Pallas kernels  251 us (98%)
  local copies, waits for them, and re-layouts  3.56 us (1%)
    pallas_call x1, Pallas kernels, body(): pl.pallas_call(functools.partial(kernel, n), out_shape=jax.ShapeDtypeStru...  251 us

profile of v4, /device:TPU:33, one launch (start us, length us, event | category | flops | bytes accessed | tf_op | source)
XLA Modules:
  0.0 255.2 jit_solution(18339075095246009225)
XLA Ops:
  0.7 251.0 %shard_map.64 = f32[640,1024]{1,0:T(8,128)} custom-call(f32[640,1024]{1,0:T(8,128)} %bitcast.3, f32[128]{0:T(128)} %occ_ref.1, f32[640]{0:T(1024)} %virt_ref.1, s32[128]{0:T(128)} %order_ref.1, s32[1]{0:T(128)S(6)} %copy.8.near_ref, s32[64]{0:T(128)} %far_ref.1), custom_call_target="tpu_custom_call" | custom-call | tf_op jit(solution)/shard_map/pallas_call | solution.py:352
  251.7 3.6 %copy.9 = f32[1,640,1024]{2,1,0:T(8,128)} copy(f32[1,640,1024]{2,1,0:T(8,128)} %bitcast.2) | data formatting | bytes 5242880

commit v5 on v4

--- a/solution.py
+++ b/solution.py
@@ -33,12 +33,13 @@
 
 def kernel(
     n,
-    own_ref, occ_ref, virt_ref, order_ref, near_ref, far_ref,
+    own_ref, occ_hbm, virt_hbm, order_hbm, near_ref, far_hbm,
     out_ref,
+    acc, occ_ref, virt_ref, order_ref, far_ref,
     transit, minor, held, own_high, own_low, high, low, amp, virt_col, virt_row, weight,
-    send_sem, recv_sem, minor_send, minor_recv, near_send, near_recv, pass_send, weight_sem, load_sem,
+    send_sem, recv_sem, minor_send, minor_recv, near_send, near_recv, pass_send, weight_sem, load_sem, small_sem, out_sem,
 ):
-    rows, depth = out_ref.shape
+    rows, depth = acc.shape
     rounds = rows // STEP
     middle = n // 2
     hops = middle // ROW
@@ -62,6 +63,12 @@
 
     load = pltpu.make_async_copy(own_ref, held.at[OWN], load_sem)
     load.start()
+    small = [
+        pltpu.make_async_copy(src, dst, small_sem.at[i])
+        for i, (src, dst) in enumerate(((occ_hbm, occ_ref), (virt_hbm, virt_ref), (order_hbm, order_ref), (far_hbm, far_ref)))
+    ]
+    for copy in small:
+        copy.start()
     barrier = pltpu.get_barrier_semaphore()
 
     def greet(device):
@@ -196,6 +203,8 @@
         def _():
             over_parts(lambda part: near_copy(part, NEXT, before).start())
 
+    for copy in small:
+        copy.wait()
     weight[OWN] = jnp.ones(weight.shape[1:], F32)
     weight[NEXT] = jnp.full(weight.shape[1:], near_ref[0].astype(F32), F32)
     weight[FAR] = jnp.full(weight.shape[1:], far_ref[lax.rem(me, middle)].astype(F32), F32)
@@ -207,7 +216,7 @@
         own_high[at], own_low[at] = split(held[OWN, at])
         high[at] = jnp.zeros((STEP, depth), BF16)
         low[at] = jnp.zeros((STEP, depth), BF16)
-        out_ref[at] = jnp.zeros((STEP, depth), F32)
+        acc[at] = jnp.zeros((STEP, depth), F32)
         return carry
 
     lax.fori_loop(0, rounds, prepare, 0)
@@ -215,8 +224,8 @@
     def energy(position):
         return occ_ref[order_ref[position]]
 
-    def compute(which, part):
-        at = pl.ds(pl.multiple_of(part * STEP, STEP), STEP)
+    def compute(which, part, final=False):
+        at = pl.ds(part * STEP, STEP) if final else band(part)
         partner = jnp.where(which == OWN, me, jnp.where(which == NEXT, after, jnp.where(which == PREV, before, opposite)))
         total = energy(me) + energy(partner)
         w = weight[which, 0:1]
@@ -234,15 +243,28 @@
         turned_high, turned_low = split((w * jnp.where(row < part * STEP, mine, 0.0)).T)
         turned = jnp.concatenate([turned_high, turned_low], axis=0)
 
-        def columns(tile, carry):
-            over = pl.ds(pl.multiple_of(tile * TILE, TILE), TILE)
+        def columns(over):
             near_high, near_low = high[at, over], low[at, over]
-            out_ref[:, over] += nn(tilde_twice, jnp.concatenate([near_high, near_low], axis=0)) + nn(tilde_low, near_high)
+            acc[:, over] += nn(tilde_twice, jnp.concatenate([near_high, near_low], axis=0)) + nn(tilde_low, near_high)
             back = nn(turned, high[:, over])
-            out_ref[at, over] -= back[:STEP] + back[STEP:] + nn(turned_high, low[:, over])
-            return carry
-
-        lax.fori_loop(0, depth // TILE, columns, 0)
+            acc[at, over] -= back[:STEP] + back[STEP:] + nn(turned_high, low[:, over])
+
+        if final:
+            for tile in range(depth // TILE):
+                columns(pl.ds(tile * TILE, TILE))
+                if tile > 0:
+                    write_out(tile - 1).start()
+        else:
+
+            def one(tile, carry):
+                columns(pl.ds(pl.multiple_of(tile * TILE, TILE), TILE))
+                return carry
+
+            lax.fori_loop(0, depth // TILE, one, 0)
+
+    def write_out(tile):
+        over = pl.ds(tile * TILE, TILE)
+        return pltpu.make_async_copy(acc.at[:, over], out_ref.at[:, over], out_sem.at[tile])
 
     own_from, near_from = 3, 24
     stride = rounds - 1
@@ -310,7 +332,9 @@
     def _():
         weight_copy().start()
 
-    lax.fori_loop(0, slots, step, 0)
+    lax.fori_loop(0, slots - 1, step, 0)
+    far_arrived(slots - 1)
+    compute(FAR, rounds - 1, final=True)
 
     def sent(slot, carry):
         far_sent(slot)
@@ -339,6 +363,24 @@
     @pl.when(~first)
     def _():
         over_parts(lambda part: near_copy(part, NEXT, before).wait_send())
+
+    tiles = depth // TILE
+    write_out(tiles - 1).start()
+    for tile in range(tiles):
+        write_out(tile).wait()
+
+
+def settle(src_ref, dst_ref, bands, in_sem, out_sem):
+    count, size = bands.shape[:2]
+    arrive = [pltpu.make_async_copy(src_ref.at[pl.ds(i * size, size)], bands.at[i], in_sem.at[i]) for i in range(count)]
+    leave = [pltpu.make_async_copy(bands.at[i], dst_ref.at[pl.ds(i * size, size)], out_sem.at[i]) for i in range(count)]
+    for copy in arrive:
+        copy.start()
+    for come, go in zip(arrive, leave):
+        come.wait()
+        go.start()
+    for copy in leave:
+        copy.wait()
 
 
 def body(slices, occ_energy, virt_energy, order, near_keep, far_keep):
@@ -346,15 +388,20 @@
     rows, depth = slices.shape[1:]
     hops = n // 2 // ROW
     rounds = rows // STEP
-    vmem = pl.BlockSpec(memory_space=pltpu.VMEM)
+    anywhere = pl.BlockSpec(memory_space=pl.ANY)
     smem = pl.BlockSpec(memory_space=pltpu.SMEM)
     dma = pltpu.SemaphoreType.DMA
     density = pl.pallas_call(
         functools.partial(kernel, n),
         out_shape=jax.ShapeDtypeStruct((rows, depth), F32),
-        in_specs=[pl.BlockSpec(memory_space=pl.ANY), smem, vmem, smem, smem, smem],
-        out_specs=vmem,
+        in_specs=[anywhere, anywhere, anywhere, anywhere, smem, anywhere],
+        out_specs=anywhere,
         scratch_shapes=[
+            pltpu.VMEM((rows, depth), F32),
+            pltpu.SMEM(occ_energy.shape, F32),
+            pltpu.VMEM(virt_energy.shape, F32),
+            pltpu.SMEM(order.shape, jnp.int32),
+            pltpu.SMEM(far_keep.shape, jnp.int32),
             pltpu.VMEM((hops - 1, rows, depth), F32),
             pltpu.VMEM((hops - 1, MINOR, depth), F32),
             pltpu.VMEM((4, rows, depth), F32),
@@ -375,11 +422,20 @@
             dma((rounds,)),
             dma((2,)),
             dma,
+            dma((4,)),
+            dma((depth // TILE,)),
         ],
         compiler_params=pltpu.CompilerParams(
             collective_id=0, has_side_effects=True, vmem_limit_bytes=62 * 1024 * 1024
         ),
     )(slices[0], occ_energy, virt_energy, order, near_keep, far_keep)
+    density = pl.pallas_call(
+        settle,
+        out_shape=jax.ShapeDtypeStruct((rows, depth), F32),
+        in_specs=[anywhere],
+        out_specs=anywhere,
+        scratch_shapes=[pltpu.VMEM((rounds, STEP, depth), F32), dma((rounds,)), dma((rounds,))],
+    )(density)
     return density[None]
 
 

time: 255 us -> 252 us (0.988)
  local copies, waits for them, and re-layouts: 3.56 us -> 0 us
    unnamed x1 -> x0, local copies, waits for them, and re-layouts: 3.56 us -> none
    pallas_call x0 -> x1, Pallas kernels: none -> 2.61 us  [body(): pl.pallas_call(settle, out_shape=jax.ShapeDtypeStruct((rows, depth), F32)...]
where the time goes in v5:
time: 252 us
  Pallas kernels  251 us (100%)
    pallas_call x1, Pallas kernels, body(): pl.pallas_call(functools.partial(kernel, n), out_shape=jax.ShapeDtypeStru...  249 us

profile of v5, /device:TPU:33, one launch (start us, length us, event | category | flops | bytes accessed | tf_op | source)
XLA Modules:
  0.0 252.1 jit_solution(1541175562496803680)
XLA Ops:
  0.7 248.8 %shard_map.64.src_ref = f32[640,1024]{1,0:T(8,128)} custom-call(f32[640,1024]{1,0:T(8,128)} %bitcast.2, f32[128]{0:T(128)} %occ_hbm.1, f32[640]{0:T(1024)} %virt_hbm.1, s32[128]{0:T(128)} %order_hbm.1, s32[1]{0:T(128)S(6)} %copy.7.near_ref, s32[64]{0:T(128)} %far_hbm.1), custom_call_target="tpu_custom_call" | custom-call | tf_op jit(solution)/shard_map/pallas_call | solution.py:394
  249.5 2.6 %shard_map.65 = f32[640,1024]{1,0:T(8,128)} custom-call(f32[640,1024]{1,0:T(8,128)} %shard_map.64.src_ref), custom_call_target="tpu_custom_call" | custom-call | tf_op jit(solution)/shard_map/pallas_call | solution.py:432

commit v6 on v5

--- a/solution.py
+++ b/solution.py
@@ -13,7 +13,7 @@
 OWN, NEXT, PREV, FAR = range(4)
 STEP = 128
 TILE = 256
-MINOR = 24
+MINOR = 16
 F32 = jnp.float32
 BF16 = jnp.bfloat16
 
@@ -85,7 +85,14 @@
     def _():
         greet(before)
 
-    pl.semaphore_wait(barrier, jnp.where(upward, jnp.where(last, 2, 1), 3))
+    closing = upward & (place == ring - 1)
+
+    @pl.when(upward & (place == hops - 2))
+    def _():
+        greet(lax.rem(me + (ring - hops + 1) * ROW, n))
+
+    heard = jnp.where(upward, jnp.where(last, 2, 1), 3) + jnp.where(closing, 1, 0)
+    pl.semaphore_wait(barrier, heard)
     load.wait()
     own = held.at[OWN]
 
@@ -136,6 +143,24 @@
                 remote(transit.at[hop - 1, at], held.at[FAR, at], *sems, onward).start()
 
         on_chunk(hop, part, from_feeder(hop), act)
+
+    def late_chunk(slot, source):
+        return upward & (lax.rem(slot, rounds) == rounds - 1) & (source == ring - 2)
+
+    def not_sent(slot):
+        hop = slot // rounds
+        return late_chunk(slot, from_feeder(hop)) & (hop > 1)
+
+    def not_received(slot):
+        hop = slot // rounds
+        return late_chunk(slot, from_feeder(hop + 1)) & (hop > 0) & (hop < hops - 1)
+
+    held_back = 2 * rounds - 1
+
+    def late_copy():
+        at = pl.ds(rows - STEP, STEP)
+        target = lax.rem(me + (hops - 1) * ROW, n)
+        return remote(transit.at[0, at], held.at[FAR, at], send_sem.at[held_back], recv_sem.at[slots - 1], target)
 
     def far_copy(slot, at):
         return remote(own.at[at], transit.at[0, at], send_sem.at[slot], recv_sem.at[slot], onward)
@@ -271,11 +296,19 @@
     near_to = near_from + 2 * rounds
 
     def step(slot, carry):
-        far_arrived(slot)
-
-        @pl.when(slot + rounds < slots)
-        def _():
-            start_hop(slot + rounds)
+        @pl.when(~not_received(slot))
+        def _():
+            far_arrived(slot)
+
+        later = slot + rounds
+
+        @pl.when((later < slots) & ~not_sent(later) & ~(closing & (later == held_back)))
+        def _():
+            start_hop(later)
+
+        @pl.when(closing & (later == slots - 1))
+        def _():
+            late_copy().start()
 
         @pl.when((lax.rem(slot, stride) == 1) & (slot < hops * stride))
         def _():
@@ -337,7 +370,10 @@
     compute(FAR, rounds - 1, final=True)
 
     def sent(slot, carry):
-        far_sent(slot)
+        @pl.when(~not_sent(slot))
+        def _():
+            far_sent(slot)
+
         return carry
 
     lax.fori_loop(0, slots, sent, 0)

time: 252 us -> 249 us (0.988)
  Pallas kernels: 251 us -> 248 us
    pallas_call x1, Pallas kernels: 249 us -> 246 us  [body(): pl.pallas_call(functools.partial(kernel, n), out_shape=jax.ShapeDtypeStru...]
where the time goes in v6:
time: 249 us
  Pallas kernels  248 us (100%)
    pallas_call x1, Pallas kernels, body(): pl.pallas_call(functools.partial(kernel, n), out_shape=jax.ShapeDtypeStru...  246 us

profile of v6, /device:TPU:33, one launch (start us, length us, event | category | flops | bytes accessed | tf_op | source)
XLA Modules:
  0.0 249.1 jit_solution(7938448292414133807)
XLA Ops:
  0.7 245.8 %shard_map.64.src_ref = f32[640,1024]{1,0:T(8,128)} custom-call(f32[640,1024]{1,0:T(8,128)} %bitcast.2, f32[128]{0:T(128)} %occ_hbm.1, f32[640]{0:T(1024)} %virt_hbm.1, s32[128]{0:T(128)} %order_hbm.1, s32[1]{0:T(128)S(6)} %copy.7.near_ref, s32[64]{0:T(128)} %far_hbm.1), custom_call_target="tpu_custom_call" | custom-call | tf_op jit(solution)/shard_map/pallas_call | solution.py:430
  246.5 2.6 %shard_map.65 = f32[640,1024]{1,0:T(8,128)} custom-call(f32[640,1024]{1,0:T(8,128)} %shard_map.64.src_ref), custom_call_target="tpu_custom_call" | custom-call | tf_op jit(solution)/shard_map/pallas_call | solution.py:468
